TPU v7x, 32 devices: a whole 2x2x4 slice. The times are simulated.
32 devices in a mesh: leaf: 8 (over z, y), front: 4 (over x, core).
Axes of the slice: x: 2, y: 2, z: 4, core: 2. Of those that a mesh axis runs over, the one named last changes fastest.
Arguments:
- app_rhs: float32 [24576, 128], P(('leaf', 'front')), may hold values from -6 to 6
- pivot_source: int32 [24576], P(('leaf', 'front')), may hold values from 0 to 24575, as said below
- row_owner: int32 [24576], P(('leaf', 'front')), may hold values from 0 to 24575, as said below
- leaf_inverse: float32 [8, 4, 384, 1536], P('leaf', 'front'), may hold values from -1 to 2, as said below
- leaf_coupling: float32 [8, 4, 384, 1024], P('leaf', 'front'), may hold values from -0.07654656 to 0.07654656
- sep1_inverse: float32 [8, 4, 128, 1024], P('leaf', 'front'), may hold values from -1 to 2, as said below
- sep1_coupling: float32 [8, 4, 128, 2048], P('leaf', 'front'), may hold values from -0.09375 to 0.09375
- sep2_inverse: float32 [8, 4, 128, 2048], P('leaf', 'front'), may hold values from -1 to 2, as said below
- sep2_coupling: float32 [8, 4, 128, 4096], P('leaf', 'front'), may hold values from -0.06629126 to 0.06629126
- sep3_inverse: float32 [8, 4, 128, 4096], P('leaf', 'front'), may hold values from -1 to 2, as said below
Outputs:
- solution: float32 [24576, 128], P(('leaf', 'front'))
Inputs may be any that keep to these rules, and one draw needn't show every extreme that they name: `pivot_source`: A permutation. Row e of pivot_rhs comes from a device's block of 768 application rows; one block's rows go to at most 16 blocks of pivot rows, at most 60 rows from one block to one block, and some pair of blocks carries exactly 60 rows. The inverse of pivot_source: pivot_source[row_owner[i]] = i. `leaf_inverse`: each front's matrix is the identity plus dense entries of magnitude at most 2 / sqrt of the front's pivot rows. `sep1_inverse`: as leaf_inverse. `sep2_inverse`: as leaf_inverse. `sep3_inverse`: as leaf_inverse.
All inputs are finite; a program needn't handle non-finite values.
Results may differ from a plain program's by a relative error of at most 0.00011.
Values sent between devices are 32-bit elements; how exact they have to be, the bound alone decides.
A program may use at most 128 MiB of HBM per device.

v0:
```python
import jax
import jax.numpy as jnp
from jax import lax
from jax.sharding import PartitionSpec as P

LEAF_PIV = 384
SEP_PIV = 128


PRECISE = lax.Precision.HIGHEST


def from_partner(block, axis, distance):
    count = lax.axis_size(axis)
    route = []
    for low in range(count):
        high = low | 1 << distance
        if high != low and high < count:
            route += [(low, high), (high, low)]
    return lax.ppermute(block, axis, route)


def ranked_slots(targets, bucket_count):
    one_hot = (targets[:, None] == jnp.arange(bucket_count, dtype=jnp.int32)[None, :]).astype(
        jnp.int32
    )
    running = jnp.cumsum(one_hot, axis=0) - one_hot
    return jnp.sum(running * one_hot, axis=1)


def move_rows(outgoing, slot_cap):
    leaves = lax.axis_size("leaf")
    fronts = lax.axis_size("front")
    rhs_count = outgoing.shape[1]
    shaped = outgoing.reshape(leaves * fronts, slot_cap, rhs_count)
    arrived = lax.all_to_all(shaped, ("leaf", "front"), split_axis=0, concat_axis=0, tiled=True)
    return arrived.reshape(leaves * fronts * slot_cap, rhs_count)


def halving_sum(shaped, bit_count):
    leaf_index = lax.axis_index("leaf")
    for bit_index in range(bit_count - 1, -1, -1):
        half_width = shaped.shape[1] // 2
        low_half = shaped[:, :half_width]
        high_half = shaped[:, half_width:]
        upper_side = leaf_index >> bit_index & 1 == 1
        kept_half = jnp.where(upper_side, high_half, low_half)
        sent_half = jnp.where(upper_side, low_half, high_half)
        shaped = kept_half + from_partner(sent_half, "leaf", bit_index)
    return shaped


def doubling_gather(shaped, bit_count):
    leaf_index = lax.axis_index("leaf")
    for bit_index in range(bit_count):
        partner_data = from_partner(shaped, "leaf", bit_index)
        upper_side = leaf_index >> bit_index & 1 == 1
        shaped = jnp.where(
            upper_side,
            jnp.concatenate([partner_data, shaped], axis=1),
            jnp.concatenate([shaped, partner_data], axis=1),
        )
    return shaped


def share_front(shaped):
    return lax.psum_scatter(shaped, "front", scatter_dimension=0, tiled=True)


def whole_front(shaped):
    return lax.all_gather(shaped, "front", axis=0, tiled=True)


def group_reduce(partial_value, bit_count, pivot_rows):
    fronts = lax.axis_size("front")
    rhs_count = partial_value.shape[1]
    shaped = partial_value.reshape(fronts, 2**bit_count, pivot_rows, rhs_count)
    shaped = halving_sum(share_front(shaped), bit_count)
    return shaped.reshape(pivot_rows, rhs_count)


def group_gather(owned_share, bit_count, pivot_rows):
    rhs_count = owned_share.shape[1]
    shaped = owned_share.reshape(1, 1, pivot_rows, rhs_count)
    shaped = whole_front(doubling_gather(shaped, bit_count))
    return shaped.reshape(-1, rhs_count)


def transposed_apply(matrix, vectors):
    return lax.dot_general(matrix, vectors, (((0,), (0,)), ((), ())), precision=PRECISE)


def per_device(
    app_rhs,
    pivot_source,
    row_owner,
    leaf_inverse,
    leaf_coupling,
    sep1_inverse,
    sep1_coupling,
    sep2_inverse,
    sep2_coupling,
    sep3_inverse,
):
    row_count = app_rhs.shape[0]
    rhs_count = app_rhs.shape[1]
    peer_count = lax.axis_size("leaf") * lax.axis_size("front")
    mean_rows = row_count // (peer_count // 2)
    slot_cap = mean_rows + max(1, mean_rows // 4)
    destination = row_owner // row_count
    send_index = destination * slot_cap + ranked_slots(destination, peer_count)
    anchor = pivot_source // row_count
    same_source = (anchor[:, None] == anchor[None, :]) & (
        pivot_source[None, :] < pivot_source[:, None]
    )
    recv_index = anchor * slot_cap + jnp.sum(same_source.astype(jnp.int32), axis=1)
    outgoing = (
        jnp.zeros((peer_count * slot_cap, rhs_count), jnp.float32).at[send_index].set(app_rhs)
    )
    ordered = move_rows(outgoing, slot_cap)[recv_index]
    inverses = (leaf_inverse[0, 0], sep1_inverse[0, 0], sep2_inverse[0, 0], sep3_inverse[0, 0])
    couplings = (leaf_coupling[0, 0], sep1_coupling[0, 0], sep2_coupling[0, 0])
    pivots = (LEAF_PIV, SEP_PIV, SEP_PIV, SEP_PIV)
    starts = (0, LEAF_PIV, LEAF_PIV + SEP_PIV, LEAF_PIV + 2 * SEP_PIV)
    solved = []
    carried = None
    for height in range(4):
        own_rhs = ordered[starts[height] : starts[height] + pivots[height]]
        if height > 0:
            own_rhs = own_rhs - group_reduce(carried, height, pivots[height])
        gathered = group_gather(own_rhs, height, pivots[height])
        forward = jnp.dot(inverses[height], gathered, precision=PRECISE)
        solved.append(forward)
        if height < 3:
            carried = transposed_apply(couplings[height], forward)
    pieces = [None, None, None, None]
    parent_sol = None
    for height in (3, 2, 1, 0):
        target = solved[height]
        if height < 3:
            target = target - jnp.dot(couplings[height], parent_sol, precision=PRECISE)
        partial_value = transposed_apply(inverses[height], target)
        owned_share = group_reduce(partial_value, height, pivots[height])
        pieces[height] = owned_share
        if height > 0:
            parent_sol = group_gather(owned_share, height, pivots[height])
    pivot_order = jnp.concatenate(pieces, axis=0)
    returning = (
        jnp.zeros((peer_count * slot_cap, rhs_count), jnp.float32).at[recv_index].set(pivot_order)
    )
    returned = move_rows(returning, slot_cap)
    return returned[send_index]


def solution(mesh):
    in_specs = (
        P(("leaf", "front"), None),
        P(("leaf", "front")),
        P(("leaf", "front")),
        P("leaf", "front", None, None),
        P("leaf", "front", None, None),
        P("leaf", "front", None, None),
        P("leaf", "front", None, None),
        P("leaf", "front", None, None),
        P("leaf", "front", None, None),
        P("leaf", "front", None, None),
    )
    out_specs = P(("leaf", "front"), None)
    return jax.shard_map(
        per_device, mesh=mesh, in_specs=in_specs, out_specs=out_specs, check_vma=False
    )
```

profile of v0, /device:TPU:0, one launch (start us, length us, event | category | flops | bytes accessed | tf_op | source)
XLA Modules:
  0.0 600.5 jit_solution(17181110750351078945)
XLA Ops:
  16.1 7.5 %all-to-all-start = ((f32[32,60,128]{2,1,0:T(8,128)}), f32[32,60,128]{2,1,0:T(8,128)}, u32[]{:S(2)}, u32[]{:S(2)}) async-start(f32[32,60,128]{2,1,0:T(8,128)} %reshape.1144), calls=%async_computation | async-start | bytes 2097152 | tf_op jit(solution)/shard_map/all_to_all | solution.py:36
  24.2 25.5 %all-to-all-done = f32[32,60,128]{2,1,0:T(8,128)} async-done(((f32[32,60,128]{2,1,0:T(8,128)}), f32[32,60,128]{2,1,0:T(8,128)}, u32[]{:S(2)}, u32[]{:S(2)}) %all-to-all-start) | async-done | bytes 983072 | tf_op jit(solution)/shard_map/all_to_all | solution.py:36
  54.3 8.7 %all-gather = f32[1536,128]{1,0:T(8,128)S(1)} all-gather(f32[384,128]{1,0:T(8,128)S(1)} %slice.125), channel_id=2, replica_groups=mesh['leaf'=8,'front'=4] {'front'}, dimensions={0}, use_global_device_ids=true | all-gather | bytes 983040 | tf_op jit(solution)/shard_map/all_gather | solution.py:71
  70.7 20.6 %reduce-scatter.8.cloned.1.call-done = f32[1,2,128,128]{3,2,1,0:T(8,128)} async-done(((f32[4,2,128,128]{3,2,1,0:T(8,128)}), f32[1,2,128,128]{3,2,1,0:T(8,128)}) %reduce-scatter.8.cloned.1.call-update) | async-done | bytes 131088 | tf_op jit(solution)/shard_map/reduce_scatter | solution.py:67
  101.8 6.5 %all_gather.22 = f32[4,2,128,128]{3,2,1,0:T(8,128)S(1)} all-gather(f32[1,2,128,128]{3,2,1,0:T(8,128)S(1)} %maximum_select_fusion.8), channel_id=1, replica_groups=mesh['leaf'=8,'front'=4] {'front'}, dimensions={0}, use_global_device_ids=true | all-gather | bytes 655360 | tf_op jit(solution)/shard_map/all_gather | solution.py:71
  115.6 25.5 %reduce-scatter.10.cloned.1.call-done = f32[1,4,128,128]{3,2,1,0:T(8,128)} async-done(((f32[4,4,128,128]{3,2,1,0:T(8,128)}), f32[1,4,128,128]{3,2,1,0:T(8,128)}) %reduce-scatter.10.cloned.1.call-update) | async-done | bytes 262160 | tf_op jit(solution)/shard_map/reduce_scatter | solution.py:67
  163.8 16.6 %all-gather.6.cloned.1.call-done = f32[4,4,128,128]{3,2,1,0:T(8,128)} async-done(((f32[1,4,128,128]{3,2,1,0:T(8,128)}), f32[4,4,128,128]{3,2,1,0:T(8,128)}) %all-gather.6.cloned.1.call-update) | async-done | bytes 1048592 | tf_op jit(solution)/shard_map/all_gather | solution.py:71
  189.8 31.3 %reduce-scatter.12.cloned.1.call-done = f32[1,8,128,128]{3,2,1,0:T(8,128)} async-done(((f32[4,8,128,128]{3,2,1,0:T(8,128)}), f32[1,8,128,128]{3,2,1,0:T(8,128)}) %reduce-scatter.12.cloned.1.call-update) | async-done | bytes 524304 | tf_op jit(solution)/shard_map/reduce_scatter | solution.py:67
  224.6 12.0 %collective-permute-done.6 = f32[1,4,128,128]{3,2,1,0:T(8,128)S(1)} collective-permute-done((f32[1,4,128,128]{3,2,1,0:T(8,128)S(1)}, f32[1,4,128,128]{3,2,1,0:T(8,128)S(1)}, u32[]{:S(2)}, u32[]{:S(2)}) %collective-permute-start.6) | collective-permute-done | bytes 262176 | tf_op jit(solution)/shard_map/ppermute | solution.py:20
  261.5 7.0 %collective-permute-done.11 = f32[1,4,128,128]{3,2,1,0:T(8,128)S(1)} collective-permute-done((f32[1,4,128,128]{3,2,1,0:T(8,128)S(1)}, f32[1,4,128,128]{3,2,1,0:T(8,128)S(1)}, u32[]{:S(2)}, u32[]{:S(2)}) %collective-permute-start.11) | collective-permute-done | bytes 262176 | tf_op jit(solution)/shard_map/ppermute | solution.py:20
  269.4 22.5 %all-gather.8.cloned.1.call-done = f32[4,8,128,128]{3,2,1,0:T(8,128)} async-done(((f32[1,8,128,128]{3,2,1,0:T(8,128)}), f32[4,8,128,128]{3,2,1,0:T(8,128)}) %all-gather.8.cloned.1.call-update) | async-done | bytes 2097168 | tf_op jit(solution)/shard_map/all_gather | solution.py:71
  291.9 5.8 fusion.4
  304.0 31.3 %reduce-scatter.14.cloned.1.call-done = f32[1,8,128,128]{3,2,1,0:T(8,128)} async-done(((f32[4,8,128,128]{3,2,1,0:T(8,128)}), f32[1,8,128,128]{3,2,1,0:T(8,128)}) %reduce-scatter.14.cloned.1.call-update) | async-done | bytes 524304 | tf_op jit(solution)/shard_map/reduce_scatter | solution.py:67
  338.8 12.0 %collective-permute-done.12 = f32[1,4,128,128]{3,2,1,0:T(8,128)S(1)} collective-permute-done((f32[1,4,128,128]{3,2,1,0:T(8,128)S(1)}, f32[1,4,128,128]{3,2,1,0:T(8,128)S(1)}, u32[]{:S(2)}, u32[]{:S(2)}) %collective-permute-start.12) | collective-permute-done | bytes 262176 | tf_op jit(solution)/shard_map/ppermute | solution.py:20
  366.7 6.2 %collective-permute-done.16 = f32[1,2,128,128]{3,2,1,0:T(8,128)S(1)} collective-permute-done((f32[1,2,128,128]{3,2,1,0:T(8,128)S(1)}, f32[1,2,128,128]{3,2,1,0:T(8,128)S(1)}, u32[]{:S(2)}, u32[]{:S(2)}) %collective-permute-start.16) | collective-permute-done | bytes 131104 | tf_op jit(solution)/shard_map/ppermute | solution.py:20
  374.8 7.1 %collective-permute-done.17 = f32[1,4,128,128]{3,2,1,0:T(8,128)S(1)} collective-permute-done((f32[1,4,128,128]{3,2,1,0:T(8,128)S(1)}, f32[1,4,128,128]{3,2,1,0:T(8,128)S(1)}, u32[]{:S(2)}, u32[]{:S(2)}) %collective-permute-start.17) | collective-permute-done | bytes 262176 | tf_op jit(solution)/shard_map/ppermute | solution.py:20
  383.1 22.2 %all-gather.10.cloned.1.call-done = f32[4,8,128,128]{3,2,1,0:T(8,128)} async-done(((f32[1,8,128,128]{3,2,1,0:T(8,128)}), f32[4,8,128,128]{3,2,1,0:T(8,128)}) %all-gather.10.cloned.1.call-update) | async-done | bytes 2097168 | tf_op jit(solution)/shard_map/all_gather | solution.py:71
  405.3 5.7 fusion.19
  415.5 24.9 %reduce-scatter.16.cloned.1.call-done = f32[1,4,128,128]{3,2,1,0:T(8,128)} async-done(((f32[4,4,128,128]{3,2,1,0:T(8,128)}), f32[1,4,128,128]{3,2,1,0:T(8,128)}) %reduce-scatter.16.cloned.1.call-update) | async-done | bytes 262160 | tf_op jit(solution)/shard_map/reduce_scatter | solution.py:67
  462.1 16.8 %all-gather.12.cloned.1.call-done = f32[4,4,128,128]{3,2,1,0:T(8,128)} async-done(((f32[1,4,128,128]{3,2,1,0:T(8,128)}), f32[4,4,128,128]{3,2,1,0:T(8,128)}) %all-gather.12.cloned.1.call-update) | async-done | bytes 1048592 | tf_op jit(solution)/shard_map/all_gather | solution.py:71
  483.7 21.7 %reduce-scatter.18.cloned.1.call-done = f32[1,2,128,128]{3,2,1,0:T(8,128)} async-done(((f32[4,2,128,128]{3,2,1,0:T(8,128)}), f32[1,2,128,128]{3,2,1,0:T(8,128)}) %reduce-scatter.18.cloned.1.call-update) | async-done | bytes 131088 | tf_op jit(solution)/shard_map/reduce_scatter | solution.py:67
  515.9 6.8 %all_gather.27 = f32[4,2,128,128]{3,2,1,0:T(8,128)S(1)} all-gather(f32[1,2,128,128]{3,2,1,0:T(8,128)S(1)} %maximum_select_fusion.17), channel_id=1, replica_groups=mesh['leaf'=8,'front'=4] {'front'}, dimensions={0}, use_global_device_ids=true | all-gather | bytes 655360 | tf_op jit(solution)/shard_map/all_gather | solution.py:71
  528.8 24.0 %reduce-scatter.20.cloned.1.call-done = f32[1,1,384,128]{3,2,1,0:T(8,128)} async-done(((f32[4,1,384,128]{3,2,1,0:T(8,128)}), f32[1,1,384,128]{3,2,1,0:T(8,128)}) %reduce-scatter.20.cloned.1.call-update) | async-done | bytes 196624 | tf_op jit(solution)/shard_map/reduce_scatter | solution.py:67
  563.8 26.2 %all-to-all-done.1 = f32[32,60,128]{2,1,0:T(8,128)} async-done(((f32[32,60,128]{2,1,0:T(8,128)}), f32[32,60,128]{2,1,0:T(8,128)}, u32[]{:S(2)}, u32[]{:S(2)}) %all-to-all-start.1) | async-done | bytes 983072 | tf_op jit(solution)/shard_map/all_to_all | solution.py:36
  (174 shorter events, 192.0 us)
Async XLA Ops:
  16.1 33.6 %all-to-all-start = ((f32[32,60,128]{2,1,0:T(8,128)}), f32[32,60,128]{2,1,0:T(8,128)}, u32[]{:S(2)}, u32[]{:S(2)}) async-start(f32[32,60,128]{2,1,0:T(8,128)} %reshape.1144), calls=%async_computation | async-start | bytes 2097152 | tf_op jit(solution)/shard_map/all_to_all | solution.py:36
  23.6 67.7 %reduce-scatter.8.cloned.1.call-start = ((), (), s32[]{:S(2)}) async-start(), calls=%async_computation.9 | async-start | bytes 655360 | tf_op jit(solution)/shard_map/reduce_scatter | solution.py:67
  70.6 70.5 %reduce-scatter.10.cloned.1.call-start = ((), (), s32[]{:S(2)}) async-start(), calls=%async_computation.10 | async-start | bytes 1310720 | tf_op jit(solution)/shard_map/reduce_scatter | solution.py:67
  115.5 64.9 %all-gather.6.cloned.1.call-start = ((), (), s32[]{:S(2)}) async-start(), calls=%async_computation.11 | async-start | bytes 1310720 | tf_op jit(solution)/shard_map/all_gather | solution.py:71
  142.1 5.1 collective-permute-start.2
  157.8 5.0 collective-permute-start.5
  163.6 57.6 %reduce-scatter.12.cloned.1.call-start = ((), (), s32[]{:S(2)}) async-start(), calls=%async_computation.12 | async-start | bytes 2621440 | tf_op jit(solution)/shard_map/reduce_scatter | solution.py:67
  189.8 102.2 %all-gather.8.cloned.1.call-start = ((), (), s32[]{:S(2)}) async-start(), calls=%async_computation.13 | async-start | bytes 2621440 | tf_op jit(solution)/shard_map/all_gather | solution.py:71
  222.2 14.5 %collective-permute-start.6 = (f32[1,4,128,128]{3,2,1,0:T(8,128)S(1)}, f32[1,4,128,128]{3,2,1,0:T(8,128)S(1)}, u32[]{:S(2)}, u32[]{:S(2)}) collective-permute-start(f32[1,4,128,128]{3,2,1,0:T(8,128)S(1)} %slice_select_fusion.1), channel_id=1, source_target_pairs={{0,16},{16,0},{4,20},{20,4},{8,24},{24,8},{12,28},{28,12},{1,17},{... | collective-permute-start | bytes 786440 | tf_op jit(solution)/shard_map/ppermute | solution.py:20
  237.7 5.0 collective-permute-start.7
  252.4 6.2 %collective-permute-start.10 = (f32[1,2,128,128]{3,2,1,0:T(8,128)S(1)}, f32[1,2,128,128]{3,2,1,0:T(8,128)S(1)}, u32[]{:S(2)}, u32[]{:S(2)}) collective-permute-start(f32[1,2,128,128]{3,2,1,0:T(8,128)S(1)} %maximum_select_fusion.11), channel_id=1, source_target_pairs={{0,8},{8,0},{4,12},{12,4},{16,24},{24,16},{20,28},{28,20},{1,9},{9... | collective-permute-start | bytes 393224 | tf_op jit(solution)/shard_map/ppermute | solution.py:20
  258.6 9.9 %collective-permute-start.11 = (f32[1,4,128,128]{3,2,1,0:T(8,128)S(1)}, f32[1,4,128,128]{3,2,1,0:T(8,128)S(1)}, u32[]{:S(2)}, u32[]{:S(2)}) collective-permute-start(f32[1,4,128,128]{3,2,1,0:T(8,128)S(1)} %maximum_select_fusion.3), channel_id=1, source_target_pairs={{0,16},{16,0},{4,20},{20,4},{8,24},{24,8},{12,28},{28,12},{1,17},{... | collective-permute-start | bytes 786440 | tf_op jit(solution)/shard_map/ppermute | solution.py:20
  269.4 65.9 %reduce-scatter.14.cloned.1.call-start = ((), (), s32[]{:S(2)}) async-start(), calls=%async_computation.14 | async-start | bytes 2621440 | tf_op jit(solution)/shard_map/reduce_scatter | solution.py:67
  303.9 101.3 %all-gather.10.cloned.1.call-start = ((), (), s32[]{:S(2)}) async-start(), calls=%async_computation.15 | async-start | bytes 2621440 | tf_op jit(solution)/shard_map/all_gather | solution.py:71
  336.3 14.5 %collective-permute-start.12 = (f32[1,4,128,128]{3,2,1,0:T(8,128)S(1)}, f32[1,4,128,128]{3,2,1,0:T(8,128)S(1)}, u32[]{:S(2)}, u32[]{:S(2)}) collective-permute-start(f32[1,4,128,128]{3,2,1,0:T(8,128)S(1)} %slice_select_fusion), channel_id=1, source_target_pairs={{0,16},{16,0},{4,20},{20,4},{8,24},{24,8},{12,28},{28,12},{1,17},{... | collective-permute-start | bytes 786440 | tf_op jit(solution)/shard_map/ppermute | solution.py:20
  351.9 5.0 collective-permute-start.13
  366.2 6.7 %collective-permute-start.16 = (f32[1,2,128,128]{3,2,1,0:T(8,128)S(1)}, f32[1,2,128,128]{3,2,1,0:T(8,128)S(1)}, u32[]{:S(2)}, u32[]{:S(2)}) collective-permute-start(f32[1,2,128,128]{3,2,1,0:T(8,128)S(1)} %maximum_select_fusion.13), channel_id=1, source_target_pairs={{0,8},{8,0},{4,12},{12,4},{16,24},{24,16},{20,28},{28,20},{1,9},{9... | collective-permute-start | bytes 393224 | tf_op jit(solution)/shard_map/ppermute | solution.py:20
  373.0 9.0 %collective-permute-start.17 = (f32[1,4,128,128]{3,2,1,0:T(8,128)S(1)}, f32[1,4,128,128]{3,2,1,0:T(8,128)S(1)}, u32[]{:S(2)}, u32[]{:S(2)}) collective-permute-start(f32[1,4,128,128]{3,2,1,0:T(8,128)S(1)} %maximum_select_fusion.5), channel_id=1, source_target_pairs={{0,16},{16,0},{4,20},{20,4},{8,24},{24,8},{12,28},{28,12},{1,17},{... | collective-permute-start | bytes 786440 | tf_op jit(solution)/shard_map/ppermute | solution.py:20
  382.8 57.6 %reduce-scatter.16.cloned.1.call-start = ((), (), s32[]{:S(2)}) async-start(), calls=%async_computation.16 | async-start | bytes 1310720 | tf_op jit(solution)/shard_map/reduce_scatter | solution.py:67
  415.5 63.4 %all-gather.12.cloned.1.call-start = ((), (), s32[]{:S(2)}) async-start(), calls=%async_computation.17 | async-start | bytes 1310720 | tf_op jit(solution)/shard_map/all_gather | solution.py:71
  441.5 5.1 collective-permute-start.18
  462.1 43.4 %reduce-scatter.18.cloned.1.call-start = ((), (), s32[]{:S(2)}) async-start(), calls=%async_computation.18 | async-start | bytes 655360 | tf_op jit(solution)/shard_map/reduce_scatter | solution.py:67
  483.7 69.1 %reduce-scatter.20.cloned.1.call-start = ((), (), s32[]{:S(2)}) async-start(), calls=%async_computation.19 | async-start | bytes 983040 | tf_op jit(solution)/shard_map/reduce_scatter | solution.py:67
  559.0 30.9 %all-to-all-start.1 = ((f32[32,60,128]{2,1,0:T(8,128)}), f32[32,60,128]{2,1,0:T(8,128)}, u32[]{:S(2)}, u32[]{:S(2)}) async-start(f32[32,60,128]{2,1,0:T(8,128)} %reshape.1171), calls=%async_computation.8 | async-start | bytes 2097152 | tf_op jit(solution)/shard_map/all_to_all | solution.py:36
  (25 other events, 359.8 us)
Sparse Core Ops, SparseCore 0:
  70.7 20.5 reduce-scatter.7
  115.6 25.4 reduce-scatter.9
  163.7 16.6 all-gather.5
  189.9 31.1 reduce-scatter.11
  269.5 22.3 all-gather.7
  304.1 31.1 reduce-scatter.13
  382.9 22.2 all-gather.9
  415.6 24.8 reduce-scatter.15
  462.2 16.6 all-gather.11
  483.8 21.6 reduce-scatter.17
  528.9 23.8 reduce-scatter.19
where the time goes:
time: 610 us; the launch traced here: 600 us
  waiting for transfers between devices  416 us (68%)
  starting transfers between devices  49.9 us (8%)
  matrix products  40.5 us (7%)
  local copies, waits for them, and re-layouts  31.8 us (5%)
  other arithmetic  26.3 us (4%)
  blocking collectives  22 us (4%)
  between operations  14.1 us (2%)
    reduce_scatter x7, waiting for transfers between devices, share_front(): return lax.psum_scatter(shaped, 'front', scatter_dimension=0, tiled=True)  179 us
    ppermute x24, waiting for transfers between devices, from_partner(): return lax.ppermute(block, axis, route)  107 us
    all_gather x4, waiting for transfers between devices, whole_front(): return lax.all_gather(shaped, 'front', axis=0, tiled=True)  78.1 us
    all_to_all x2, waiting for transfers between devices, move_rows(): lax.all_to_all(shaped, ('leaf', 'front'), split_axis=0, concat_axis=0, ti...  51.7 us
    ppermute x24, starting transfers between devices, from_partner(): return lax.ppermute(block, axis, route)  36.9 us
    all_gather x3, blocking collectives, whole_front(): return lax.all_gather(shaped, 'front', axis=0, tiled=True)  22 us
    reshape x7, local copies, waits for them, and re-layouts, group_reduce(): partial_value.reshape(fronts, 2 ** bit_count, pivot_rows, rhs_count)  15.2 us
    dot_general x7, matrix products, transposed_apply(): lax.dot_general(matrix, vectors, (((0,), (0,)), ((), ())), precision=PREC...  14.5 us
  transfers between devices with their start and end apart: 37, of which 37 were waited for; matrix products, arithmetic and copies ran while one was open for 0% of the time, Pallas kernels for 0%

commit v1 on v0

v1 whole, which is shorter than its diff:
```python
import functools

import jax
import jax.numpy as jnp
from jax import lax
from jax.experimental import pallas as pl
from jax.experimental.pallas import tpu as pltpu
from jax.sharding import PartitionSpec as P

LEAF_PIV = 384
SEP_PIV = 128
BLK = 128
CHUNK = 4
MESH = pl.DeviceIdType.MESH


def ranked_slots(targets, bucket_count):
    one_hot = (targets[:, None] == jnp.arange(bucket_count, dtype=jnp.int32)[None, :]).astype(
        jnp.int32
    )
    running = jnp.cumsum(one_hot, axis=0) - one_hot
    return jnp.sum(running * one_hot, axis=1)


def move_rows(outgoing, slot_cap):
    leaves = lax.axis_size("leaf")
    fronts = lax.axis_size("front")
    rhs_count = outgoing.shape[1]
    shaped = outgoing.reshape(leaves * fronts, slot_cap, rhs_count)
    arrived = lax.all_to_all(shaped, ("leaf", "front"), split_axis=0, concat_axis=0, tiled=True)
    return arrived.reshape(leaves * fronts * slot_cap, rhs_count)


def bit_of(value, place):
    return lax.rem(lax.div(value, jnp.int32(2**place)), jnp.int32(2))


def stripe_orders(front_bits, height):
    front = [("front", place) for place in range(front_bits)]
    leaf = [("leaf", place) for place in range(height)]
    first = front + leaf
    second = front[:1] + leaf[:1] + front[1:] + leaf[1:]
    return (first, second)


def split(value):
    high = value.astype(jnp.bfloat16)
    return high, (value - high.astype(jnp.float32)).astype(jnp.bfloat16)


def product(left, right, right_axis):
    dims = (((1,), (right_axis,)), ((), ()))
    dot = functools.partial(lax.dot_general, dimension_numbers=dims, preferred_element_type=jnp.float32)
    left_high, left_low = left
    right_high, right_low = split(right)
    return dot(left_high, right_high) + (dot(left_low, right_high) + dot(left_high, right_low))


def solve_kernel(front_bits, stripe_rows, sizes, *refs):
    rhs_ref, *weights_hbm = refs[:8]
    out_ref = refs[8]
    weights = refs[9:16]
    buffers = refs[16:]
    stripes = len(stripe_rows)
    pos = 0

    def take(count):
        nonlocal pos
        pos += count
        return buffers[pos - count : pos]

    up = [take(stripes) for _ in range(4)]
    down = [None] + [take(stripes) for _ in range(3)]
    partial = take(stripes)
    up_recv = [None] + [take(stripes) for _ in range(3)]
    down_recv = [take(stripes) for _ in range(4)]
    solved = take(4)
    load_sems, send_sems, recv_sems = take(3)
    used = [0]

    leaf = lax.axis_index("leaf")
    front = lax.axis_index("front")
    here = {"leaf": leaf, "front": front}

    def partner(bit):
        axis, place = bit
        mine = bit_of(here[axis], place)
        other = here[axis] + (1 - 2 * mine) * 2**place
        return (other, front) if axis == "leaf" else (leaf, other)

    all_bits = [("front", place) for place in range(front_bits)] + [("leaf", place) for place in range(3)]
    barrier = pltpu.get_barrier_semaphore()
    for bit in all_bits:
        pl.semaphore_signal(barrier, inc=1, device_id=partner(bit), device_id_type=MESH)
    loads = []
    for index in range(7):
        load = pltpu.make_async_copy(weights_hbm[index], weights[index], load_sems.at[index])
        load.start()
        loads.append(load)
    pl.semaphore_wait(barrier, len(all_bits))

    def unit(height):
        return LEAF_PIV // BLK if height == 0 else 1

    def slot_of(block, height, stripe):
        piece = unit(height)
        place, rest = (block, 0) if piece == 1 else (lax.div(block, jnp.int32(piece)), lax.rem(block, jnp.int32(piece)))
        order = stripe_orders(front_bits, height)[stripe]
        slot = 0
        for axis, at in order:
            slot = slot * 2 + bit_of(place, at + height if axis == "front" else at)
        return slot * piece + rest

    def remote(source, target, bit):
        index = used[0]
        used[0] += 1
        copy = pltpu.make_async_remote_copy(
            src_ref=source,
            dst_ref=target,
            send_sem=send_sems.at[index],
            recv_sem=recv_sems.at[index],
            device_id=partner(bit),
            device_id_type=MESH,
        )
        copy.start()
        return copy

    def own_slots(height):
        out = []
        for stripe in range(stripes):
            slot = 0
            for axis, at in stripe_orders(front_bits, height)[stripe]:
                slot = slot * 2 + bit_of(here[axis], at)
            out.append(slot * unit(height))
        return out

    def reduce_group(height, bufs, recvs):
        piece = unit(height)
        orders = stripe_orders(front_bits, height)
        depth = len(orders[0])
        bases = [jnp.int32(0)] * stripes
        half = 2**depth * piece
        offset = 0
        for step in range(depth + 1):
            copies = []
            whole, half = half, half // 2
            for stripe in range(stripes):
                if step > 0:
                    pending[stripe].wait()
                    keep = bases[stripe]

                    def add(index, carry, stripe=stripe, keep=keep, prior=prior):
                        bufs[stripe][keep + index] += recvs[stripe][prior + index]
                        return carry

                    lax.fori_loop(0, whole, add, 0)
                if step < depth:
                    bit = orders[stripe][step]
                    mine = bit_of(here[bit[0]], bit[1])
                    away = bases[stripe] + (1 - mine) * half
                    bases[stripe] = bases[stripe] + mine * half
                    copies.append(
                        remote(bufs[stripe].at[pl.ds(away, half)], recvs[stripe].at[pl.ds(offset, half)], bit)
                    )
            pending, prior = copies, offset
            offset += half

    def gather_group(height, bufs):
        piece = unit(height)
        orders = stripe_orders(front_bits, height)
        depth = len(orders[0])
        bases = own_slots(height)
        size = piece
        pending = None
        for step in range(depth, -1, -1):
            copies = []
            for stripe in range(stripes):
                if pending is not None:
                    pending[stripe].wait()
                if step > 0:
                    bit = orders[stripe][step - 1]
                    span = pl.ds(bases[stripe], size)
                    copies.append(remote(bufs[stripe].at[span], bufs[stripe].at[span], bit))
                    bases[stripe] = bases[stripe] - bit_of(here[bit[0]], bit[1]) * size
            pending = copies
            size *= 2

    def apply_rows(weight, bufs, height):
        rows = weight.shape[0]
        count = sizes[height] // BLK

        def body(index, total):
            parts = []
            for step in range(CHUNK):
                block = index * CHUNK + step
                parts.append(
                    jnp.concatenate([bufs[s][slot_of(block, height, s)] for s in range(stripes)], axis=0)
                )
            left = split(jnp.concatenate(parts, axis=1))
            start = pl.multiple_of(index * (CHUNK * BLK), CHUNK * BLK)
            return total + product(left, weight[:, pl.ds(start, CHUNK * BLK)], 1)

        return lax.fori_loop(0, count // CHUNK, body, jnp.zeros((BLK, rows), jnp.float32))

    def apply_cols(weight, vector, bufs, height):
        count = sizes[height] // BLK
        left = split(vector)

        def body(index, carry):
            start = pl.multiple_of(index * (CHUNK * BLK), CHUNK * BLK)
            result = product(left, weight[:, pl.ds(start, CHUNK * BLK)], 0)
            for step in range(CHUNK):
                block = index * CHUNK + step
                low = 0
                for s in range(stripes):
                    bufs[s][slot_of(block, height, s)] = result[
                        low : low + stripe_rows[s], step * BLK : (step + 1) * BLK
                    ]
                    low += stripe_rows[s]
            return carry

        lax.fori_loop(0, count // CHUNK, body, 0)

    def own_block(bufs, slots, part):
        return jnp.concatenate([bufs[s][slots[s] + part] for s in range(stripes)], axis=0)

    def set_block(bufs, slots, part, value):
        low = 0
        for s in range(stripes):
            bufs[s][slots[s] + part] = value[low : low + stripe_rows[s]]
            low += stripe_rows[s]

    inverses = (weights[0], weights[2], weights[4], weights[6])
    couplings = (weights[1], weights[3], weights[5])
    starts = (0, LEAF_PIV, LEAF_PIV + SEP_PIV, LEAF_PIV + 2 * SEP_PIV)
    for height in range(4):
        slots = own_slots(height)
        if height > 0:
            reduce_group(height, partial, up_recv[height])
        for part in range(unit(height)):
            low = starts[height] + part * BLK
            value = rhs_ref[low : low + BLK, :].T
            if height > 0:
                value = value - own_block(partial, slots, part)
            set_block(up[height], slots, part, value)
        gather_group(height, up[height])
        loads[2 * height].wait()
        forward = apply_rows(inverses[height], up[height], height)
        solved[height][...] = forward
        if height < 3:
            loads[2 * height + 1].wait()
            apply_cols(couplings[height], forward, partial, height + 1)
    for height in (3, 2, 1, 0):
        target = solved[height][...]
        if height < 3:
            target = target - apply_rows(couplings[height], down[height + 1], height + 1)
        apply_cols(inverses[height], target, partial, height)
        reduce_group(height, partial, down_recv[height])
        slots = own_slots(height)
        for part in range(unit(height)):
            low = starts[height] + part * BLK
            value = own_block(partial, slots, part)
            out_ref[low : low + BLK, :] = value.T
            if height > 0:
                set_block(down[height], slots, part, value)
        if height > 0:
            gather_group(height, down[height])


def solve(ordered, weights):
    leaves = lax.axis_size("leaf")
    fronts = lax.axis_size("front")
    front_bits = fronts.bit_length() - 1
    rhs_count = ordered.shape[1]
    stripe_rows = (rhs_count // 2, rhs_count // 2)
    sizes = tuple(w.shape[1] for w in (weights[0], weights[2], weights[4], weights[6]))
    scratch = [pltpu.VMEM(w.shape, jnp.float32) for w in weights]

    def stripe_buffers(blocks):
        return [pltpu.VMEM((blocks, rows, BLK), jnp.float32) for rows in stripe_rows]

    counts = [size // BLK for size in sizes]
    copies = 0
    for height in range(4):
        copies += (2 if height == 0 else 4) * (front_bits + height) * len(stripe_rows)
    for blocks in counts + counts[1:] + [max(counts)] + counts[1:] + counts:
        scratch += stripe_buffers(blocks)
    scratch += [pltpu.VMEM((rhs_count, rows), jnp.float32) for rows in (LEAF_PIV, SEP_PIV, SEP_PIV, SEP_PIV)]
    scratch += [
        pltpu.SemaphoreType.DMA((7,)),
        pltpu.SemaphoreType.DMA((copies,)),
        pltpu.SemaphoreType.DMA((copies,)),
    ]
    vmem = pl.BlockSpec(memory_space=pltpu.VMEM)
    return pl.pallas_call(
        functools.partial(solve_kernel, front_bits, stripe_rows, sizes),
        out_shape=jax.ShapeDtypeStruct(ordered.shape, jnp.float32),
        in_specs=[vmem] + [pl.BlockSpec(memory_space=pl.ANY)] * 7,
        out_specs=vmem,
        scratch_shapes=scratch,
        compiler_params=pltpu.CompilerParams(
            collective_id=0, has_side_effects=True, vmem_limit_bytes=66 * 1024 * 1000
        ),
    )(ordered, *weights)


def per_device(
    app_rhs,
    pivot_source,
    row_owner,
    leaf_inverse,
    leaf_coupling,
    sep1_inverse,
    sep1_coupling,
    sep2_inverse,
    sep2_coupling,
    sep3_inverse,
):
    row_count = app_rhs.shape[0]
    rhs_count = app_rhs.shape[1]
    peer_count = lax.axis_size("leaf") * lax.axis_size("front")
    mean_rows = row_count // (peer_count // 2)
    slot_cap = mean_rows + max(1, mean_rows // 4)
    destination = row_owner // row_count
    send_index = destination * slot_cap + ranked_slots(destination, peer_count)
    anchor = pivot_source // row_count
    same_source = (anchor[:, None] == anchor[None, :]) & (
        pivot_source[None, :] < pivot_source[:, None]
    )
    recv_index = anchor * slot_cap + jnp.sum(same_source.astype(jnp.int32), axis=1)
    outgoing = (
        jnp.zeros((peer_count * slot_cap, rhs_count), jnp.float32).at[send_index].set(app_rhs)
    )
    ordered = move_rows(outgoing, slot_cap)[recv_index]
    weights = [
        w[0, 0]
        for w in (
            leaf_inverse,
            leaf_coupling,
            sep1_inverse,
            sep1_coupling,
            sep2_inverse,
            sep2_coupling,
            sep3_inverse,
        )
    ]
    pivot_order = solve(ordered, weights)
    returning = (
        jnp.zeros((peer_count * slot_cap, rhs_count), jnp.float32).at[recv_index].set(pivot_order)
    )
    returned = move_rows(returning, slot_cap)
    return returned[send_index]


def solution(mesh):
    in_specs = (
        P(("leaf", "front"), None),
        P(("leaf", "front")),
        P(("leaf", "front")),
        P("leaf", "front", None, None),
        P("leaf", "front", None, None),
        P("leaf", "front", None, None),
        P("leaf", "front", None, None),
        P("leaf", "front", None, None),
        P("leaf", "front", None, None),
        P("leaf", "front", None, None),
    )
    out_specs = P(("leaf", "front"), None)
    return jax.shard_map(
        per_device, mesh=mesh, in_specs=in_specs, out_specs=out_specs, check_vma=False
    )
```

time: 610 us -> 288 us (0.47); the launches traced: 600 us -> 288 us
  waiting for transfers between devices: 416 us -> 51.2 us
  Pallas kernels: 0 us -> 203 us
  matrix products: 40.5 us -> 0 us
  starting transfers between devices: 49.9 us -> 11.8 us
  other arithmetic: 26.3 us -> 3.87 us
  blocking collectives: 22 us -> 0 us
  local copies, waits for them, and re-layouts: 31.8 us -> 17.3 us
  between operations: 14.1 us -> 0.14 us
    pallas_call x0 -> x1, Pallas kernels: none -> 203 us  [solve(): pl.pallas_call(functools.partial(solve_kernel, front_bits, stripe_rows, s...]
    reduce_scatter x7 -> x0, waiting for transfers between devices: 179 us -> none  [share_front(): return lax.psum_scatter(shaped, 'front', scatter_dimension=0, tiled=True)]
    ppermute x24 -> x0, waiting for transfers between devices: 107 us -> none  [from_partner(): return lax.ppermute(block, axis, route)]
    all_gather x4 -> x0, waiting for transfers between devices: 78.1 us -> none  [whole_front(): return lax.all_gather(shaped, 'front', axis=0, tiled=True)]
    dot_general x14 -> x0, matrix products: 40.5 us -> none  [the longest x7 14.5 us: transposed_apply(): lax.dot_general(matrix, vectors, (((0,), (0,)), ((), ())), precision=PREC...]
    ppermute x24 -> x0, starting transfers between devices: 36.9 us -> none  [from_partner(): return lax.ppermute(block, axis, route)]
    all_gather x3 -> x0, blocking collectives: 22 us -> none  [whole_front(): return lax.all_gather(shaped, 'front', axis=0, tiled=True)]
    reshape x7 -> x0, local copies, waits for them, and re-layouts: 15.2 us -> none  [group_reduce(): partial_value.reshape(fronts, 2 ** bit_count, pivot_rows, rhs_count)]
  transfers between devices with their start and end apart: 37 -> 2, of which waited for: 37 -> 2; matrix products, arithmetic and copies ran while one was open for 0% -> 0% of each run, Pallas kernels for 0% -> 0%
where the time goes in v1:
time: 288 us
  Pallas kernels  203 us (70%)
  waiting for transfers between devices  51.2 us (18%)
  local copies, waits for them, and re-layouts  17.3 us (6%)
  starting transfers between devices  11.8 us (4%)
  other arithmetic  3.87 us (1%)
    pallas_call x1, Pallas kernels, solve(): pl.pallas_call(functools.partial(solve_kernel, front_bits, stripe_rows, s...  203 us
    all_to_all x2, waiting for transfers between devices, move_rows(): lax.all_to_all(shaped, ('leaf', 'front'), split_axis=0, concat_axis=0, ti...  51.2 us
    all_to_all x2, starting transfers between devices, move_rows(): lax.all_to_all(shaped, ('leaf', 'front'), split_axis=0, concat_axis=0, ti...  11.8 us
  transfers between devices with their start and end apart: 2, of which 2 were waited for; matrix products, arithmetic and copies ran while one was open for 0% of the time, Pallas kernels for 0%

profile of v1, /device:TPU:0, one launch (start us, length us, event | category | flops | bytes accessed | tf_op | source)
XLA Modules:
  0.0 287.5 jit_solution(7881882480401179641)
XLA Ops:
  0.0 0.7 add_select_fusion
  0.7 1.7 reduce-window.6
  2.5 0.3 slice_reduce_fusion
  2.7 0.1 fusion.6
  2.9 0.7 compare_select_fusion
  3.6 0.0 copy-start
  3.6 4.8 %scatter_custom_fusion = f32[1920,128]{1,0:T(8,128)S(1)} fusion(s32[768]{0:T(1024)S(1)} %compare_select_fusion, f32[768,128]{1,0:T(8,128)} %param.10, f32[]{:T(128)} %constant.19.clone.1), kind=kCustom, calls=%fused_computation.7 | custom fusion | bytes 983552 | tf_op jit(solution)/shard_map/scatter | solution.py:332
  8.4 1.1 reshape.33
  9.5 0.0 copy-done.1
  9.5 7.3 %all-to-all-start = ((f32[32,60,128]{2,1,0:T(8,128)}), f32[32,60,128]{2,1,0:T(8,128)S(1)}, u32[]{:S(2)}, u32[]{:S(2)}) async-start(f32[32,60,128]{2,1,0:T(8,128)} %reshape.33), calls=%async_computation | async-start | bytes 2097152 | tf_op jit(solution)/shard_map/all_to_all | solution.py:30
  16.8 0.0 copy-done
  16.8 0.5 convert_reduce_fusion
  17.4 0.0 copy-start.3
  17.4 0.6 copy-done.3
  18.0 25.0 %all-to-all-done = f32[32,60,128]{2,1,0:T(8,128)S(1)} async-done(((f32[32,60,128]{2,1,0:T(8,128)}), f32[32,60,128]{2,1,0:T(8,128)S(1)}, u32[]{:S(2)}, u32[]{:S(2)}) %all-to-all-start) | async-done | bytes 983072 | tf_op jit(solution)/shard_map/all_to_all | solution.py:30
  43.0 0.1 reshape.34
  43.1 2.3 gather_fusion
  45.4 203.2 %shard_map.100 = f32[768,128]{1,0:T(8,128)} custom-call(f32[768,128]{1,0:T(8,128)} %gather_fusion, f32[384,1536]{1,0:T(8,128)} %bitcast.29, f32[384,1024]{1,0:T(8,128)} %bitcast.32, f32[128,1024]{1,0:T(8,128)} %bitcast.35, f32[128,2048]{1,0:T(8,128)} %bitcast.33, f32[128,2048]{1,0:T(8,128)} %bitcast.34, f32[128,4096]{1,0:T(8,128)} %bitcast.30, ...), custom_call_target="tpu_custom_call" | custom-call | tf_op jit(solution)/shard_map/pallas_call | solution.py:295
  248.6 4.8 %scatter_custom_fusion.1 = f32[1920,128]{1,0:T(8,128)S(1)} fusion(s32[768]{0:T(1024)} %copy-done.3, f32[768,128]{1,0:T(8,128)} %shard_map.100, f32[]{:T(128)} %constant.19.clone.1), kind=kCustom, calls=%fused_computation.5 | custom fusion | bytes 983552 | tf_op jit(solution)/shard_map/scatter | solution.py:349
  253.4 1.1 reshape.35
  254.4 4.5 %all-to-all-start.1 = ((f32[32,60,128]{2,1,0:T(8,128)}), f32[32,60,128]{2,1,0:T(8,128)S(1)}, u32[]{:S(2)}, u32[]{:S(2)}) async-start(f32[32,60,128]{2,1,0:T(8,128)} %reshape.35), calls=%async_computation.1 | async-start | bytes 2097152 | tf_op jit(solution)/shard_map/all_to_all | solution.py:30
  259.0 26.2 %all-to-all-done.1 = f32[32,60,128]{2,1,0:T(8,128)S(1)} async-done(((f32[32,60,128]{2,1,0:T(8,128)}), f32[32,60,128]{2,1,0:T(8,128)S(1)}, u32[]{:S(2)}, u32[]{:S(2)}) %all-to-all-start.1) | async-done | bytes 983072 | tf_op jit(solution)/shard_map/all_to_all | solution.py:30
  285.1 0.1 reshape.36
  285.2 2.3 gather_fusion.1
  (9 shorter events, 0.1 us)
Async XLA Ops:
  3.6 5.9 %copy-start.1 = (s32[768]{0:T(1024)}, s32[768]{0:T(1024)S(1)}, u32[]{:S(2)}) copy-start(s32[768]{0:T(1024)S(1)} %compare_select_fusion) | copy-start | bytes 9220
  3.6 13.2 %copy-start = (s32[768]{0:T(1024)S(1)}, s32[768]{0:T(1024)}, u32[]{:S(2)}) copy-start(s32[768]{0:T(1024)} %param.11) | copy-start | bytes 9220
  9.5 33.5 %all-to-all-start = ((f32[32,60,128]{2,1,0:T(8,128)}), f32[32,60,128]{2,1,0:T(8,128)S(1)}, u32[]{:S(2)}, u32[]{:S(2)}) async-start(f32[32,60,128]{2,1,0:T(8,128)} %reshape.33), calls=%async_computation | async-start | bytes 2097152 | tf_op jit(solution)/shard_map/all_to_all | solution.py:30
  17.4 0.6 copy-start.3
  248.5 10.4 %copy-start.2 = (s32[768]{0:T(1024)S(1)}, s32[768]{0:T(1024)}, u32[]{:S(2)}) copy-start(s32[768]{0:T(1024)} %copy-done.1) | copy-start | bytes 9220
  254.4 30.7 %all-to-all-start.1 = ((f32[32,60,128]{2,1,0:T(8,128)}), f32[32,60,128]{2,1,0:T(8,128)S(1)}, u32[]{:S(2)}, u32[]{:S(2)}) async-start(f32[32,60,128]{2,1,0:T(8,128)} %reshape.35), calls=%async_computation.1 | async-start | bytes 2097152 | tf_op jit(solution)/shard_map/all_to_all | solution.py:30

commit v2 on v1

--- a/solution.py
+++ b/solution.py
@@ -11,6 +11,7 @@
 SEP_PIV = 128
 BLK = 128
 CHUNK = 4
+STRIPES = 4
 MESH = pl.DeviceIdType.MESH
 
 
@@ -104,11 +105,13 @@
 
     def slot_of(block, height, stripe):
         piece = unit(height)
-        place, rest = (block, 0) if piece == 1 else (lax.div(block, jnp.int32(piece)), lax.rem(block, jnp.int32(piece)))
-        order = stripe_orders(front_bits, height)[stripe]
+        static = isinstance(block, int)
+        place, rest = divmod(block, piece) if static else (block, 0)
+        order = stripe_orders(front_bits, height)[stripe % 2]
         slot = 0
         for axis, at in order:
-            slot = slot * 2 + bit_of(place, at + height if axis == "front" else at)
+            at = at + height if axis == "front" else at
+            slot = slot * 2 + (place >> at & 1 if static else bit_of(place, at))
         return slot * piece + rest
 
     def remote(source, target, bit):
@@ -129,12 +132,12 @@
         out = []
         for stripe in range(stripes):
             slot = 0
-            for axis, at in stripe_orders(front_bits, height)[stripe]:
+            for axis, at in stripe_orders(front_bits, height)[stripe % 2]:
                 slot = slot * 2 + bit_of(here[axis], at)
             out.append(slot * unit(height))
         return out
 
-    def reduce_group(height, bufs, recvs):
+    def reduce_group(height, bufs, recvs, middle):
         piece = unit(height)
         orders = stripe_orders(front_bits, height)
         depth = len(orders[0])
@@ -155,17 +158,19 @@
 
                     lax.fori_loop(0, whole, add, 0)
                 if step < depth:
-                    bit = orders[stripe][step]
+                    bit = orders[stripe % 2][step]
                     mine = bit_of(here[bit[0]], bit[1])
                     away = bases[stripe] + (1 - mine) * half
                     bases[stripe] = bases[stripe] + mine * half
                     copies.append(
                         remote(bufs[stripe].at[pl.ds(away, half)], recvs[stripe].at[pl.ds(offset, half)], bit)
                     )
+            if step == 0:
+                middle()
             pending, prior = copies, offset
             offset += half
 
-    def gather_group(height, bufs):
+    def gather_group(height, bufs, middle):
         piece = unit(height)
         orders = stripe_orders(front_bits, height)
         depth = len(orders[0])
@@ -174,52 +179,89 @@
         pending = None
         for step in range(depth, -1, -1):
             copies = []
+            if step == 0:
+                middle()
             for stripe in range(stripes):
                 if pending is not None:
                     pending[stripe].wait()
                 if step > 0:
-                    bit = orders[stripe][step - 1]
+                    bit = orders[stripe % 2][step - 1]
                     span = pl.ds(bases[stripe], size)
                     copies.append(remote(bufs[stripe].at[span], bufs[stripe].at[span], bit))
                     bases[stripe] = bases[stripe] - bit_of(here[bit[0]], bit[1]) * size
             pending = copies
             size *= 2
 
-    def apply_rows(weight, bufs, height):
-        rows = weight.shape[0]
-        count = sizes[height] // BLK
-
-        def body(index, total):
-            parts = []
-            for step in range(CHUNK):
-                block = index * CHUNK + step
-                parts.append(
-                    jnp.concatenate([bufs[s][slot_of(block, height, s)] for s in range(stripes)], axis=0)
-                )
+    def splits(height):
+        return unit(height) == 1 and 2**height % CHUNK == 0
+
+    def chunks(height, side, body, carry):
+        count = sizes[height] // BLK // CHUNK
+        if unit(height) > 1:
+            for index in range(count):
+                slots = [
+                    [slot_of(index * CHUNK + step, height, kind) for kind in range(2)] for step in range(CHUNK)
+                ]
+                carry = body(index * CHUNK * BLK, slots, carry)
+            return carry
+
+        def visit(index, carry):
+            if side is not None:
+                run = 2**height // CHUNK
+                index = lax.div(index, jnp.int32(run)) * (2 * run) + side * run + lax.rem(index, jnp.int32(run))
+            bases = [slot_of(index * CHUNK, height, kind) for kind in range(2)]
+            slots = [[bases[kind] + slot_of(step, height, kind) for kind in range(2)] for step in range(CHUNK)]
+            return body(pl.multiple_of(index * (CHUNK * BLK), CHUNK * BLK), slots, carry)
+
+        return lax.fori_loop(0, count if side is None else count // 2, visit, carry)
+
+    def apply_rows(weight, bufs, height, side, total):
+        def body(start, slots, total):
+            parts = [
+                jnp.concatenate([bufs[s][slots[step][s % 2]] for s in range(stripes)], axis=0)
+                for step in range(CHUNK)
+            ]
             left = split(jnp.concatenate(parts, axis=1))
-            start = pl.multiple_of(index * (CHUNK * BLK), CHUNK * BLK)
             return total + product(left, weight[:, pl.ds(start, CHUNK * BLK)], 1)
 
-        return lax.fori_loop(0, count // CHUNK, body, jnp.zeros((BLK, rows), jnp.float32))
-
-    def apply_cols(weight, vector, bufs, height):
-        count = sizes[height] // BLK
+        return chunks(height, side, body, total)
+
+    def apply_cols(weight, vector, bufs, height, side):
         left = split(vector)
 
-        def body(index, carry):
-            start = pl.multiple_of(index * (CHUNK * BLK), CHUNK * BLK)
+        def body(start, slots, carry):
             result = product(left, weight[:, pl.ds(start, CHUNK * BLK)], 0)
             for step in range(CHUNK):
-                block = index * CHUNK + step
                 low = 0
                 for s in range(stripes):
-                    bufs[s][slot_of(block, height, s)] = result[
-                        low : low + stripe_rows[s], step * BLK : (step + 1) * BLK
-                    ]
+                    bufs[s][slots[step][s % 2]] = result[low : low + stripe_rows[s], step * BLK : (step + 1) * BLK]
                     low += stripe_rows[s]
             return carry
 
-        lax.fori_loop(0, count // CHUNK, body, 0)
+        chunks(height, side, body, 0)
+
+    core = bit_of(front, 0)
+
+    def reduced(weight, vector, height, recvs):
+        if splits(height):
+            apply_cols(weight, vector, partial, height, 1 - core)
+            reduce_group(
+                height, partial, recvs, lambda: apply_cols(weight, vector, partial, height, core)
+            )
+        else:
+            apply_cols(weight, vector, partial, height, None)
+            reduce_group(height, partial, recvs, lambda: None)
+
+    def gathered_rows(weight, bufs, height, ready):
+        totals = [jnp.zeros((BLK, weight.shape[0]), jnp.float32)]
+
+        def own_side():
+            ready()
+            if splits(height):
+                totals.append(apply_rows(weight, bufs, height, core, totals[-1]))
+
+        gather_group(height, bufs, own_side)
+        return apply_rows(weight, bufs, height, 1 - core if splits(height) else None, totals[-1])
 
     def own_block(bufs, slots, part):
         return jnp.concatenate([bufs[s][slots[s] + part] for s in range(stripes)], axis=0)
@@ -236,26 +278,20 @@
     for height in range(4):
         slots = own_slots(height)
         if height > 0:
-            reduce_group(height, partial, up_recv[height])
+            loads[2 * height - 1].wait()
+            reduced(couplings[height - 1], solved[height - 1][...], height, up_recv[height])
         for part in range(unit(height)):
             low = starts[height] + part * BLK
             value = rhs_ref[low : low + BLK, :].T
             if height > 0:
                 value = value - own_block(partial, slots, part)
             set_block(up[height], slots, part, value)
-        gather_group(height, up[height])
-        loads[2 * height].wait()
-        forward = apply_rows(inverses[height], up[height], height)
-        solved[height][...] = forward
-        if height < 3:
-            loads[2 * height + 1].wait()
-            apply_cols(couplings[height], forward, partial, height + 1)
+        solved[height][...] = gathered_rows(inverses[height], up[height], height, loads[2 * height].wait)
     for height in (3, 2, 1, 0):
         target = solved[height][...]
         if height < 3:
-            target = target - apply_rows(couplings[height], down[height + 1], height + 1)
-        apply_cols(inverses[height], target, partial, height)
-        reduce_group(height, partial, down_recv[height])
+            target = target - gathered_rows(couplings[height], down[height + 1], height + 1, lambda: None)
+        reduced(inverses[height], target, height, down_recv[height])
         slots = own_slots(height)
         for part in range(unit(height)):
             low = starts[height] + part * BLK
@@ -263,8 +299,6 @@
             out_ref[low : low + BLK, :] = value.T
             if height > 0:
                 set_block(down[height], slots, part, value)
-        if height > 0:
-            gather_group(height, down[height])
 
 
 def solve(ordered, weights):
@@ -272,7 +306,7 @@
     fronts = lax.axis_size("front")
     front_bits = fronts.bit_length() - 1
     rhs_count = ordered.shape[1]
-    stripe_rows = (rhs_count // 2, rhs_count // 2)
+    stripe_rows = (rhs_count // STRIPES,) * STRIPES
     sizes = tuple(w.shape[1] for w in (weights[0], weights[2], weights[4], weights[6]))
     scratch = [pltpu.VMEM(w.shape, jnp.float32) for w in weights]
 

time: 288 us -> 267 us (0.927)
  Pallas kernels: 203 us -> 183 us
    pallas_call x1, Pallas kernels: 203 us -> 183 us  [solve(): pl.pallas_call(functools.partial(solve_kernel, front_bits, stripe_rows, s...]
where the time goes in v2:
time: 267 us; the launch traced here: 266 us
  Pallas kernels  183 us (69%)
  waiting for transfers between devices  51 us (19%)
  local copies, waits for them, and re-layouts  17.3 us (6%)
  starting transfers between devices  11.3 us (4%)
  other arithmetic  3.87 us (1%)
    pallas_call x1, Pallas kernels, solve(): pl.pallas_call(functools.partial(solve_kernel, front_bits, stripe_rows, s...  183 us
    all_to_all x2, waiting for transfers between devices, move_rows(): lax.all_to_all(shaped, ('leaf', 'front'), split_axis=0, concat_axis=0, ti...  51 us
    all_to_all x2, starting transfers between devices, move_rows(): lax.all_to_all(shaped, ('leaf', 'front'), split_axis=0, concat_axis=0, ti...  11.3 us
  transfers between devices with their start and end apart: 2, of which 2 were waited for; matrix products, arithmetic and copies ran while one was open for 0% of the time, Pallas kernels for 0%

profile of v2, /device:TPU:0, one launch (start us, length us, event | category | flops | bytes accessed | tf_op | source)
XLA Modules:
  0.0 266.2 jit_solution(7236590248063267619)
XLA Ops:
  0.0 0.7 add_select_fusion
  0.7 1.7 reduce-window.6
  2.5 0.3 slice_reduce_fusion
  2.7 0.1 fusion.6
  2.9 0.7 compare_select_fusion
  3.6 0.0 copy-start
  3.6 4.8 %scatter_custom_fusion = f32[1920,128]{1,0:T(8,128)S(1)} fusion(s32[768]{0:T(1024)S(1)} %compare_select_fusion, f32[768,128]{1,0:T(8,128)} %param.10, f32[]{:T(128)} %constant.19.clone.1), kind=kCustom, calls=%fused_computation.7 | custom fusion | bytes 983552 | tf_op jit(solution)/shard_map/scatter | solution.py:366
  8.4 1.1 reshape.33
  9.5 0.0 copy-done.1
  9.5 7.5 %all-to-all-start = ((f32[32,60,128]{2,1,0:T(8,128)}), f32[32,60,128]{2,1,0:T(8,128)S(1)}, u32[]{:S(2)}, u32[]{:S(2)}) async-start(f32[32,60,128]{2,1,0:T(8,128)} %reshape.33), calls=%async_computation | async-start | bytes 2097152 | tf_op jit(solution)/shard_map/all_to_all | solution.py:31
  17.0 0.0 copy-done
  17.0 0.5 convert_reduce_fusion
  17.6 0.0 copy-start.3
  17.6 0.6 copy-done.3
  18.2 24.8 %all-to-all-done = f32[32,60,128]{2,1,0:T(8,128)S(1)} async-done(((f32[32,60,128]{2,1,0:T(8,128)}), f32[32,60,128]{2,1,0:T(8,128)S(1)}, u32[]{:S(2)}, u32[]{:S(2)}) %all-to-all-start) | async-done | bytes 983072 | tf_op jit(solution)/shard_map/all_to_all | solution.py:31
  43.0 0.1 reshape.34
  43.1 2.3 gather_fusion
  45.4 182.5 %shard_map.100 = f32[768,128]{1,0:T(8,128)} custom-call(f32[768,128]{1,0:T(8,128)} %gather_fusion, f32[384,1536]{1,0:T(8,128)} %bitcast.29, f32[384,1024]{1,0:T(8,128)} %bitcast.32, f32[128,1024]{1,0:T(8,128)} %bitcast.35, f32[128,2048]{1,0:T(8,128)} %bitcast.33, f32[128,2048]{1,0:T(8,128)} %bitcast.34, f32[128,4096]{1,0:T(8,128)} %bitcast.30, ...), custom_call_target="tpu_custom_call" | custom-call | tf_op jit(solution)/shard_map/pallas_call | solution.py:329
  227.9 4.8 %scatter_custom_fusion.1 = f32[1920,128]{1,0:T(8,128)S(1)} fusion(s32[768]{0:T(1024)} %copy-done.3, f32[768,128]{1,0:T(8,128)} %shard_map.100, f32[]{:T(128)} %constant.19.clone.1), kind=kCustom, calls=%fused_computation.5 | custom fusion | bytes 983552 | tf_op jit(solution)/shard_map/scatter | solution.py:383
  232.7 1.1 reshape.35
  233.8 3.8 %all-to-all-start.1 = ((f32[32,60,128]{2,1,0:T(8,128)}), f32[32,60,128]{2,1,0:T(8,128)S(1)}, u32[]{:S(2)}, u32[]{:S(2)}) async-start(f32[32,60,128]{2,1,0:T(8,128)} %reshape.35), calls=%async_computation.1 | async-start | bytes 2097152 | tf_op jit(solution)/shard_map/all_to_all | solution.py:31
  237.6 26.2 %all-to-all-done.1 = f32[32,60,128]{2,1,0:T(8,128)S(1)} async-done(((f32[32,60,128]{2,1,0:T(8,128)}), f32[32,60,128]{2,1,0:T(8,128)S(1)}, u32[]{:S(2)}, u32[]{:S(2)}) %all-to-all-start.1) | async-done | bytes 983072 | tf_op jit(solution)/shard_map/all_to_all | solution.py:31
  263.8 0.1 reshape.36
  263.9 2.3 gather_fusion.1
  (9 shorter events, 0.1 us)
Async XLA Ops:
  3.6 5.9 %copy-start.1 = (s32[768]{0:T(1024)}, s32[768]{0:T(1024)S(1)}, u32[]{:S(2)}) copy-start(s32[768]{0:T(1024)S(1)} %compare_select_fusion) | copy-start | bytes 9220
  3.6 13.4 %copy-start = (s32[768]{0:T(1024)S(1)}, s32[768]{0:T(1024)}, u32[]{:S(2)}) copy-start(s32[768]{0:T(1024)} %param.11) | copy-start | bytes 9220
  9.5 33.5 %all-to-all-start = ((f32[32,60,128]{2,1,0:T(8,128)}), f32[32,60,128]{2,1,0:T(8,128)S(1)}, u32[]{:S(2)}, u32[]{:S(2)}) async-start(f32[32,60,128]{2,1,0:T(8,128)} %reshape.33), calls=%async_computation | async-start | bytes 2097152 | tf_op jit(solution)/shard_map/all_to_all | solution.py:31
  17.6 0.6 copy-start.3
  227.9 9.7 %copy-start.2 = (s32[768]{0:T(1024)S(1)}, s32[768]{0:T(1024)}, u32[]{:S(2)}) copy-start(s32[768]{0:T(1024)} %copy-done.1) | copy-start | bytes 9220
  233.8 30.0 %all-to-all-start.1 = ((f32[32,60,128]{2,1,0:T(8,128)}), f32[32,60,128]{2,1,0:T(8,128)S(1)}, u32[]{:S(2)}, u32[]{:S(2)}) async-start(f32[32,60,128]{2,1,0:T(8,128)} %reshape.35), calls=%async_computation.1 | async-start | bytes 2097152 | tf_op jit(solution)/shard_map/all_to_all | solution.py:31

commit v3 on v2

--- a/solution.py
+++ b/solution.py
@@ -11,7 +11,7 @@
 SEP_PIV = 128
 BLK = 128
 CHUNK = 4
-STRIPES = 4
+STRIPES = 8
 MESH = pl.DeviceIdType.MESH
 
 

time: 267 us -> 263 us (0.985)
  Pallas kernels: 183 us -> 179 us
    pallas_call x1, Pallas kernels: 183 us -> 179 us  [solve(): pl.pallas_call(functools.partial(solve_kernel, front_bits, stripe_rows, s...]
where the time goes in v3:
time: 263 us; the launch traced here: 262 us
  Pallas kernels  179 us (68%)
  waiting for transfers between devices  51 us (19%)
  local copies, waits for them, and re-layouts  17.5 us (7%)
  starting transfers between devices  11.1 us (4%)
  other arithmetic  3.87 us (1%)
    pallas_call x1, Pallas kernels, solve(): pl.pallas_call(functools.partial(solve_kernel, front_bits, stripe_rows, s...  179 us
    all_to_all x2, waiting for transfers between devices, move_rows(): lax.all_to_all(shaped, ('leaf', 'front'), split_axis=0, concat_axis=0, ti...  51 us
    all_to_all x2, starting transfers between devices, move_rows(): lax.all_to_all(shaped, ('leaf', 'front'), split_axis=0, concat_axis=0, ti...  11.1 us
  transfers between devices with their start and end apart: 2, of which 2 were waited for; matrix products, arithmetic and copies ran while one was open for 0% of the time, Pallas kernels for 0%

profile of v3, /device:TPU:0, one launch (start us, length us, event | category | flops | bytes accessed | tf_op | source)
XLA Modules:
  0.0 262.2 jit_solution(1258930866032873491)
XLA Ops:
  0.0 0.7 add_select_fusion
  0.7 1.7 reduce-window.6
  2.5 0.3 slice_reduce_fusion
  2.7 0.1 fusion.6
  2.9 0.7 compare_select_fusion
  3.6 0.0 copy-start
  3.6 4.8 %scatter_custom_fusion = f32[1920,128]{1,0:T(8,128)S(1)} fusion(s32[768]{0:T(1024)S(1)} %compare_select_fusion, f32[768,128]{1,0:T(8,128)} %param.10, f32[]{:T(128)} %constant.19.clone.1), kind=kCustom, calls=%fused_computation.7 | custom fusion | bytes 983552 | tf_op jit(solution)/shard_map/scatter | solution.py:366
  8.4 1.1 reshape.33
  9.5 0.0 copy-done.1
  9.5 7.5 %all-to-all-start = ((f32[32,60,128]{2,1,0:T(8,128)}), f32[32,60,128]{2,1,0:T(8,128)S(1)}, u32[]{:S(2)}, u32[]{:S(2)}) async-start(f32[32,60,128]{2,1,0:T(8,128)} %reshape.33), calls=%async_computation | async-start | bytes 2097152 | tf_op jit(solution)/shard_map/all_to_all | solution.py:31
  17.0 0.0 copy-done
  17.0 0.5 convert_reduce_fusion
  17.6 0.0 copy-start.3
  17.6 0.6 copy-done.3
  18.2 24.8 %all-to-all-done = f32[32,60,128]{2,1,0:T(8,128)S(1)} async-done(((f32[32,60,128]{2,1,0:T(8,128)}), f32[32,60,128]{2,1,0:T(8,128)S(1)}, u32[]{:S(2)}, u32[]{:S(2)}) %all-to-all-start) | async-done | bytes 983072 | tf_op jit(solution)/shard_map/all_to_all | solution.py:31
  43.0 0.1 reshape.34
  43.1 2.3 gather_fusion
  45.4 178.6 %shard_map.100 = f32[768,128]{1,0:T(8,128)} custom-call(f32[768,128]{1,0:T(8,128)} %gather_fusion, f32[384,1536]{1,0:T(8,128)} %bitcast.29, f32[384,1024]{1,0:T(8,128)} %bitcast.32, f32[128,1024]{1,0:T(8,128)} %bitcast.35, f32[128,2048]{1,0:T(8,128)} %bitcast.33, f32[128,2048]{1,0:T(8,128)} %bitcast.34, f32[128,4096]{1,0:T(8,128)} %bitcast.30, ...), custom_call_target="tpu_custom_call" | custom-call | tf_op jit(solution)/shard_map/pallas_call | solution.py:329
  223.9 5.0 %scatter_custom_fusion.1 = f32[1920,128]{1,0:T(8,128)S(1)} fusion(s32[768]{0:T(1024)} %copy-done.3, f32[768,128]{1,0:T(8,128)} %shard_map.100, f32[]{:T(128)} %constant.19.clone.1), kind=kCustom, calls=%fused_computation.5 | custom fusion | bytes 983552 | tf_op jit(solution)/shard_map/scatter | solution.py:383
  229.0 1.1 reshape.35
  230.0 3.6 %all-to-all-start.1 = ((f32[32,60,128]{2,1,0:T(8,128)}), f32[32,60,128]{2,1,0:T(8,128)S(1)}, u32[]{:S(2)}, u32[]{:S(2)}) async-start(f32[32,60,128]{2,1,0:T(8,128)} %reshape.35), calls=%async_computation.1 | async-start | bytes 2097152 | tf_op jit(solution)/shard_map/all_to_all | solution.py:31
  233.7 26.2 %all-to-all-done.1 = f32[32,60,128]{2,1,0:T(8,128)S(1)} async-done(((f32[32,60,128]{2,1,0:T(8,128)}), f32[32,60,128]{2,1,0:T(8,128)S(1)}, u32[]{:S(2)}, u32[]{:S(2)}) %all-to-all-start.1) | async-done | bytes 983072 | tf_op jit(solution)/shard_map/all_to_all | solution.py:31
  259.9 0.1 reshape.36
  259.9 2.3 gather_fusion.1
  (9 shorter events, 0.1 us)
Async XLA Ops:
  3.6 5.9 %copy-start.1 = (s32[768]{0:T(1024)}, s32[768]{0:T(1024)S(1)}, u32[]{:S(2)}) copy-start(s32[768]{0:T(1024)S(1)} %compare_select_fusion) | copy-start | bytes 9220
  3.6 13.4 %copy-start = (s32[768]{0:T(1024)S(1)}, s32[768]{0:T(1024)}, u32[]{:S(2)}) copy-start(s32[768]{0:T(1024)} %param.11) | copy-start | bytes 9220
  9.5 33.5 %all-to-all-start = ((f32[32,60,128]{2,1,0:T(8,128)}), f32[32,60,128]{2,1,0:T(8,128)S(1)}, u32[]{:S(2)}, u32[]{:S(2)}) async-start(f32[32,60,128]{2,1,0:T(8,128)} %reshape.33), calls=%async_computation | async-start | bytes 2097152 | tf_op jit(solution)/shard_map/all_to_all | solution.py:31
  17.6 0.6 copy-start.3
  223.9 9.7 %copy-start.2 = (s32[768]{0:T(1024)S(1)}, s32[768]{0:T(1024)}, u32[]{:S(2)}) copy-start(s32[768]{0:T(1024)} %copy-done.1) | copy-start | bytes 9220
  230.0 29.8 %all-to-all-start.1 = ((f32[32,60,128]{2,1,0:T(8,128)}), f32[32,60,128]{2,1,0:T(8,128)S(1)}, u32[]{:S(2)}, u32[]{:S(2)}) async-start(f32[32,60,128]{2,1,0:T(8,128)} %reshape.35), calls=%async_computation.1 | async-start | bytes 2097152 | tf_op jit(solution)/shard_map/all_to_all | solution.py:31
